TPU v7x, 8 devices: a whole 2x2x1 slice. The times are simulated.
8 devices in a mesh: dp: 2 (over z, y), sp: 4 (over x, core).
Axes of the slice: x: 2, y: 2, z: 1, core: 2. Of those that a mesh axis runs over, the one named last changes fastest.
Arguments:
- tokens: bfloat16 [16384, 384], P(('dp', 'sp')), parts along dimension 0
- grad_out: bfloat16 [16384, 384], P(('dp', 'sp')), parts along dimension 0
- ln_gain: float32 [384], replicated
- ln_bias: float32 [384], replicated
- w_qkv: bfloat16 [384, 1152], replicated
- w_out: bfloat16 [384, 384], replicated
- temperature: float32 [8], replicated
Outputs:
- output 1: bfloat16 [16384, 384], P(('dp', 'sp')), parts along dimension 0
- output 2: bfloat16 [16384, 384], P(('dp', 'sp')), parts along dimension 0
- output 3: float32 [768, 1152], P(('dp', 'sp')), parts along dimension 0
- output 4: float32 [768, 384], P(('dp', 'sp')), parts along dimension 0
- output 5: float32 [768], P('dp'), parts along dimension 0
- output 6: float32 [768], P('dp'), parts along dimension 0
- output 7: float32 [16], P('dp'), parts along dimension 0
There are 2 independent parts. A program takes and returns all parts, laid end to end along the dimension named above; an argument that names none is the same for every part.
All inputs are finite; a program needn't handle non-finite values.
Results may differ from a plain program's by a relative error of at most 0.00136218.
Values are sent between devices in bfloat16 or wider.
A program may use at most 1 GiB of HBM per device.

v0:
```python
import jax
import jax.numpy as jnp
from jax import lax
from jax.sharding import PartitionSpec as P


def layer_norm(x_f32, ln_gain, ln_bias):
    row_mean = jnp.mean(x_f32, axis=-1, keepdims=True)
    centered = x_f32 - row_mean
    row_var = jnp.mean(centered * centered, axis=-1, keepdims=True)
    return centered * lax.rsqrt(row_var + 1e-6) * ln_gain + ln_bias


def attn_probs(gram_sum, q_sq, k_sq, value_a11):
    cosine = gram_sum / (jnp.sqrt(q_sq)[..., :, None] * jnp.sqrt(k_sq)[..., None, :])
    return jax.nn.softmax(value_a11[..., None, None] * cosine, axis=-1)


def project(x_rows, ln_gain, ln_bias, w_qkv, num_heads):
    ln_value, ln_vjp = jax.vjp(layer_norm, x_rows.astype(jnp.float32), ln_gain, ln_bias)
    normed = ln_value.astype(jnp.bfloat16)
    qkv_act = jnp.dot(normed, w_qkv, preferred_element_type=jnp.float32).astype(jnp.bfloat16)
    qkv_heads = qkv_act.reshape(x_rows.shape[0], 3, num_heads, -1)
    return ln_vjp, normed, qkv_heads[:, 0], qkv_heads[:, 1], qkv_heads[:, 2]


def apply_attn(v_heads, attn_weights):
    attn_out = jnp.einsum('nhj,hij->nhi', v_heads, attn_weights, preferred_element_type=jnp.float32)
    return attn_out.astype(jnp.bfloat16).reshape(v_heads.shape[0], -1)


def solution(mesh):
    row_spec = P(('dp', 'sp'), None)
    part_spec = P('dp')
    full_spec = P()

    def local_step(x_loc, dy_loc, ln_gain, ln_bias, w_qkv, w_out, value_a11):
        local_rows, model_width = x_loc.shape
        num_heads = value_a11.shape[0]
        fwd_act = project(x_loc, ln_gain, ln_bias, w_qkv, num_heads)
        q_heads, k_heads, v_heads = fwd_act[2], fwd_act[3], fwd_act[4]
        gram_part = jnp.einsum('nhi,nhj->hij', q_heads, k_heads, preferred_element_type=jnp.float32)
        qsq_part = jnp.einsum('nhi,nhi->hi', q_heads, q_heads, preferred_element_type=jnp.float32)
        ksq_part = jnp.einsum('nhj,nhj->hj', k_heads, k_heads, preferred_element_type=jnp.float32)
        gram_sum, q_sq, k_sq = lax.psum((gram_part, qsq_part, ksq_part), 'sp')
        attn_weights = attn_probs(gram_sum, q_sq, k_sq, value_a11).astype(jnp.bfloat16)
        attn_out = apply_attn(v_heads, attn_weights)
        out_proj = jnp.dot(attn_out, w_out, preferred_element_type=jnp.float32)
        out_tokens = (x_loc.astype(jnp.float32) + out_proj).astype(jnp.bfloat16)

        x_again, gram_kept, qsq_kept, ksq_kept = lax.optimization_barrier((x_loc, gram_sum, q_sq, k_sq))
        ln_vjp, normed, q_heads, k_heads, v_heads = project(x_again, ln_gain, ln_bias, w_qkv, num_heads)
        attn_f32, probs_vjp = jax.vjp(attn_probs, gram_kept, qsq_kept, ksq_kept, value_a11)
        attn_weights = attn_f32.astype(jnp.bfloat16)
        attn_out = apply_attn(v_heads, attn_weights)
        wout_part = jnp.einsum('nc,nd->cd', attn_out, dy_loc, preferred_element_type=jnp.float32)
        grad_w_out = lax.psum_scatter(wout_part, 'sp', scatter_dimension=0, tiled=True)
        d_attn = jnp.einsum('nd,cd->nc', dy_loc, w_out, preferred_element_type=jnp.float32)
        d_attn = d_attn.astype(jnp.bfloat16).reshape(local_rows, num_heads, -1)
        probs_part = jnp.einsum('nhi,nhj->hij', d_attn, v_heads, preferred_element_type=jnp.float32)
        d_probs = lax.psum(probs_part, 'sp')
        d_gram, d_qsq, d_ksq, value_a16 = probs_vjp(d_probs)
        d_gram_bf = d_gram.astype(jnp.bfloat16)
        d_q = jnp.einsum('hij,nhj->nhi', d_gram_bf, k_heads, preferred_element_type=jnp.float32) + 2.0 * q_heads * d_qsq
        d_k = jnp.einsum('hij,nhi->nhj', d_gram_bf, q_heads, preferred_element_type=jnp.float32) + 2.0 * k_heads * d_ksq
        d_v = jnp.einsum('hij,nhi->nhj', attn_weights, d_attn, preferred_element_type=jnp.float32)
        d_qkv = jnp.stack([d_q, d_k, d_v], axis=1).astype(jnp.bfloat16).reshape(local_rows, 3 * model_width)
        wqkv_part = jnp.einsum('nc,nk->ck', normed, d_qkv, preferred_element_type=jnp.float32)
        grad_w_qkv = lax.psum_scatter(wqkv_part, 'sp', scatter_dimension=0, tiled=True)
        d_normed = jnp.einsum('nk,ck->nc', d_qkv, w_qkv, preferred_element_type=jnp.float32)
        d_x, gain_part, bias_part = ln_vjp(d_normed)
        grad_gain, grad_bias = lax.psum((gain_part, bias_part), 'sp')
        grad_tokens = (dy_loc.astype(jnp.float32) + d_x).astype(jnp.bfloat16)
        return out_tokens, grad_tokens, grad_w_qkv, grad_w_out, grad_gain, grad_bias, value_a16

    return jax.shard_map(local_step, mesh=mesh,
                         in_specs=(row_spec, row_spec, full_spec, full_spec, full_spec, full_spec, full_spec),
                         out_specs=(row_spec, row_spec, row_spec, row_spec, part_spec, part_spec, part_spec),
                         check_vma=False)
```

profile of v0, /device:TPU:0, one launch (start us, length us, event | category | flops | bytes accessed | tf_op | source)
XLA Modules:
  0.0 142.1 jit_solution(13206388353259776942)
XLA Ops:
  7.2 0.0 copy-start
  7.2 0.0 copy-start.1
  7.2 0.0 copy-start.10
  7.2 0.0 copy-start.12
  7.2 0.0 all-reduce.5.cloned.1.call-start
  7.3 1.9 %convert_reduce_fusion = f32[2048]{0:T(1024)S(1)} fusion(bf16[2048,384]{1,0:T(8,128)(2,1)} %param.7), kind=kLoop, calls=%fused_computation.7 | loop fusion | flops 1570816 | bytes 1581056 | tf_op jit(solution)/shard_map/jvp()/reduce_sum | solution.py:8
  9.2 2.2 %fusion.13 = f32[2048]{0:T(1024)S(1)} fusion(bf16[2048,384]{1,0:T(8,128)(2,1)} %param.7, f32[2048]{0:T(1024)S(1)} %broadcast_multiply_fusion.1), kind=kLoop, calls=%fused_computation.22 | loop fusion | flops 3143680 | bytes 1589248 | tf_op jit(solution)/shard_map/jvp()/reduce_sum | solution.py:10
  11.4 0.0 copy-done
  11.4 0.0 copy-done.1
  11.4 0.0 copy-done.10
  11.4 0.0 copy-done.12
  11.4 3.4 %convolution_convert_fusion.1 = bf16[2048,1152]{0,1:T(8,128)(2,1)S(1)} fusion(bf16[384,1152]{1,0:T(8,128)(2,1)S(1)} %copy-done, bf16[2048,384]{1,0:T(8,128)(2,1)S(1)} %copy-done.1, f32[384]{0:T(512)S(1)} %copy-done.12, f32[384]{0:T(512)S(1)} %copy-done.10, f32[2048]{0:T(1024)S(1)} %add_rsqrt_fusion, f32[2048]{0:T(1024)S(1)} %broadcast_multiply_fusion.1), kind=kOutput, calls=%fused_computation.3 | convolution fusion | flops 1819017216 | bytes 7195648 | tf_op jit(solution)/shard_map/dot_general | solution.py:22
  14.8 0.0 copy-start.4
  14.8 0.0 copy-start.9
  14.8 2.1 %copy-done.4 = bf16[2048,1152]{0,1:T(8,128)(2,1)} copy-done((bf16[2048,1152]{0,1:T(8,128)(2,1)}, bf16[2048,1152]{0,1:T(8,128)(2,1)S(1)}, u32[]{:S(2)}) %copy-start.4) | copy-done | bytes 4718616
  16.9 1.2 fusion.28
  18.2 0.0 all-reduce.5.cloned.1.call-update
  18.2 0.0 all-reduce.7.cloned.1.call-start
  18.2 0.0 copy-done.9
  18.2 0.0 copy-start.5
  18.3 3.7 %convolution_convert_fusion.4 = bf16[2048,384]{0,1:T(8,128)(2,1)} fusion(bf16[2048,384]{1,0:T(8,128)(2,1)} %param.8, bf16[384,384]{1,0:T(8,128)(2,1)S(1)} %copy-done.9), kind=kOutput, calls=%fused_computation.40 | convolution fusion | flops 604766208 | bytes 3440640 | tf_op jit(solution)/shard_map/nd,cd->nc/dot_general | solution.py:58
  22.0 0.0 copy-done.5
  22.0 0.0 copy-start.11
  22.0 0.7 fusion.23
  22.7 9.1 %all-reduce.1 = (f32[8,48]{1,0:T(8,128)S(1)}, f32[8,48]{1,0:T(8,128)S(1)}) all-reduce(f32[8,48]{1,0:T(8,128)S(1)} %get-tuple-element.18, f32[8,48]{1,0:T(8,128)S(1)} %get-tuple-element.17), channel_id=1, replica_groups=mesh['dp'=2,'sp'=4] {'sp'}, use_global_device_ids=true, to_apply=%region_4.0 | all-reduce | flops 768 | bytes 6144 | tf_op jit(solution)/shard_map/psum | solution.py:45
  31.7 15.9 %all-reduce.5.cloned.1.call-done = f32[8,48,48]{2,1,0:T(8,128)} async-done(((f32[8,48,48]{2,1,0:T(8,128)}), f32[8,48,48]{2,1,0:T(8,128)}) %all-reduce.5.cloned.1.call-update) | async-done | bytes 73744 | tf_op jit(solution)/shard_map/psum | solution.py:45
  47.6 0.0 copy-start.8
  47.6 0.4 convert_reduce_fusion.1
  48.0 0.8 fusion.17
  48.8 0.0 copy-done.11
  48.8 0.0 copy-done.8
  48.8 2.0 %fusion.69 = (f32[8,48]{1,0:T(8,128)S(1)}, f32[8,48,48]{2,1,0:T(8,128)S(1)}) fusion(f32[8]{0:T(128)S(1)} %copy-done.11, f32[8,48,48]{2,1,0:T(8,128)S(1)} %copy-done.8, f32[8,48]{1,0:T(8,128)S(1)} %sqrt.15, f32[8,48]{1,0:T(8,128)S(1)} %sqrt.14), kind=kOutput, calls=%fused_computation.99 | output fusion | flops 92207 | bytes 152096 | tf_op jit(solution)/shard_map/jvp()/sub | solution.py:16
  50.8 4.9 %convolution_convert_fusion = bf16[2048,1152]{0,1:T(8,128)(2,1)} fusion(bf16[384,1152]{1,0:T(8,128)(2,1)S(1)} %copy-done, bf16[2048,384]{1,0:T(8,128)(2,1)S(1)} %copy-done.1, f32[2048]{0:T(1024)S(1)} %fusion.50, f32[2048]{0:T(1024)S(1)} %broadcast_multiply_fusion, f32[384]{0:T(512)S(1)} %copy-done.12, f32[384]{0:T(512)S(1)} %copy-done.10), kind=kOutput, calls=%fused_computation.2 | convolution fusion | flops 1819017216 | bytes 7195648 | tf_op jit(solution)/shard_map/dot_general | solution.py:22
  55.7 4.0 %convolution_convert_fusion.2 = bf16[8,48,2048]{2,1,0:T(8,128)(2,1)} fusion(bf16[2048,3,8,48]{0,3,2,1:T(8,128)(2,1)} %bitcast.85, f32[8,48]{1,0:T(8,128)S(1)} %get-tuple-element.30, f32[8]{0:T(128)S(1)} %copy-done.11, f32[8,48,48]{2,1,0:T(8,128)S(1)} %copy-done.8, f32[8,48]{1,0:T(8,128)S(1)} %sqrt.15, f32[8,48]{1,0:T(8,128)S(1)} %sqrt.14), kind=kOutput, calls=%fused_computation.38 | convolution fusion | flops 76394928 | bytes 3224096 | tf_op jit(solution)/shard_map/nhj,hij->nhi/dot_general | solution.py:28
  59.7 3.1 %fusion.35 = f32[8,48,48]{2,1,0:T(8,128)} fusion(bf16[2048,8,48]{0,2,1:T(8,128)(2,1)} %bitcast.76, bf16[2048,3,8,48]{0,3,2,1:T(8,128)(2,1)} %bitcast.86), kind=kOutput, calls=%fused_computation.56 | convolution fusion | flops 75497472 | bytes 3219456 | tf_op jit(solution)/shard_map/nhi,nhj->hij/dot_general | solution.py:60
  62.9 0.0 all-reduce.7.cloned.1.call-update
  62.9 0.0 reduce-scatter.5.cloned.1.call-start
  62.9 3.7 %fusion.70 = f32[384,384]{1,0:T(8,128)} fusion(bf16[2048,384]{0,1:T(8,128)(2,1)} %bitcast.83, bf16[2048,384]{1,0:T(8,128)(2,1)} %param.8), kind=kOutput, calls=%fused_computation.100 | convolution fusion | flops 603979776 | bytes 3735552 | tf_op jit(solution)/shard_map/nc,nd->cd/dot_general | solution.py:56
  66.6 4.2 %fusion.24 = bf16[2048,1,8,48]{0,3,2,1:T(8,128)(2,1)} fusion(bf16[2048,8,48]{0,2,1:T(8,128)(2,1)} %bitcast.77, f32[8,48]{1,0:T(8,128)S(1)} %get-tuple-element.30, f32[8]{0:T(128)S(1)} %copy-done.11, f32[8,48,48]{2,1,0:T(8,128)S(1)} %copy-done.8, f32[8,48]{1,0:T(8,128)S(1)} %sqrt.15, f32[8,48]{1,0:T(8,128)S(1)} %sqrt.14), kind=kOutput, calls=%fused_computation.42 | convolution fusion | flops 76394928 | bytes 3224096 | tf_op jit(solution)/shard_map/hij,nhi->nhj/dot_general | solution.py:66
  70.8 0.0 reduce-scatter.5.cloned.1.call-update
  70.8 0.2 reduce-scatter.3.cloned.1.call-start
  71.1 18.4 %all-reduce.7.cloned.1.call-done = f32[8,48,48]{2,1,0:T(8,128)} async-done(((f32[8,48,48]{2,1,0:T(8,128)}), f32[8,48,48]{2,1,0:T(8,128)}) %all-reduce.7.cloned.1.call-update) | async-done | bytes 73744 | tf_op jit(solution)/shard_map/psum | solution.py:61
  89.5 1.2 multiply_reduce_fusion.3
  90.7 1.2 fusion.46
  91.8 0.8 multiply_reduce_fusion.2
  92.6 2.9 %fusion.26 = bf16[2048,1,8,48]{0,3,2,1:T(8,128)(2,1)S(1)} fusion(f32[8,48]{1,0:T(8,128)S(1)} %get-tuple-element.33, bf16[2048,3,8,48]{0,3,2,1:T(8,128)(2,1)} %bitcast.87, f32[8,48,48]{2,1,0:T(8,128)S(1)} %get-tuple-element.29, f32[8,48]{1,0:T(8,128)S(1)} %sqrt.15, f32[8,48]{1,0:T(8,128)S(1)} %sqrt.14, f32[8]{0:T(128)S(1)} %copy-done.11), kind=kOutput, calls=%fused_computation.44 | convolution fusion | flops 79503360 | bytes 4796960 | tf_op jit(solution)/shard_map/hij,nhi->nhj/dot_general | solution.py:65
  95.5 0.0 copy-start.3
  95.6 2.8 %fusion.25 = bf16[2048,1,8,48]{0,3,2,1:T(8,128)(2,1)S(1)} fusion(f32[8,48]{1,0:T(8,128)S(1)} %get-tuple-element.34, bf16[2048,3,8,48]{0,3,2,1:T(8,128)(2,1)} %bitcast.88, f32[8,48,48]{2,1,0:T(8,128)S(1)} %get-tuple-element.29, f32[8,48]{1,0:T(8,128)S(1)} %sqrt.15, f32[8,48]{1,0:T(8,128)S(1)} %sqrt.14, f32[8]{0:T(128)S(1)} %copy-done.11), kind=kOutput, calls=%fused_computation.43 | convolution fusion | flops 79503360 | bytes 4796960 | tf_op jit(solution)/shard_map/hij,nhj->nhi/dot_general | solution.py:64
  98.3 0.0 copy-done.3
  98.3 0.6 pad_maximum_fusion
  98.9 0.0 copy-start.6
  98.9 2.2 %copy-done.6 = bf16[2048,3,8,48]{0,3,2,1:T(8,128)(2,1)} copy-done((bf16[2048,3,8,48]{0,3,2,1:T(8,128)(2,1)}, bf16[2048,3,8,48]{0,3,2,1:T(8,128)(2,1)S(1)}, u32[]{:S(2)}) %copy-start.6) | copy-done | bytes 4718616
  101.1 4.2 %fusion.63 = f32[384,1152]{1,0:T(8,128)} fusion(bf16[2048,1152]{0,1:T(8,128)(2,1)S(1)} %bitcast.81, bf16[2048,384]{1,0:T(8,128)(2,1)S(1)} %copy-done.1, f32[2048]{0:T(1024)S(1)} %fusion.50, f32[2048]{0:T(1024)S(1)} %broadcast_multiply_fusion, f32[384]{0:T(512)S(1)} %copy-done.12, f32[384]{0:T(512)S(1)} %copy-done.10), kind=kOutput, calls=%fused_computation.95 | convolution fusion | flops 1816657920 | bytes 8080384 | tf_op jit(solution)/shard_map/nc,nk->ck/dot_general | solution.py:68
  105.2 0.0 reduce-scatter.3.cloned.1.call-update
  105.3 1.5 %fusion.68 = f32[8,48]{1,0:T(8,128)S(1)} fusion(f32[8,48,48]{2,1,0:T(8,128)S(1)} %copy-done.8, f32[8,48]{1,0:T(8,128)S(1)} %sqrt.13, f32[8,48]{1,0:T(8,128)S(1)} %sqrt.12, f32[8]{0:T(128)S(1)} %copy-done.11), kind=kOutput, calls=%fused_computation.98 | output fusion | flops 92207 | bytes 78368 | tf_op jit(solution)/shard_map/sub | solution.py:16
  106.8 4.0 %convolution_convert_fusion.5 = bf16[8,48,2048]{2,1,0:T(8,128)(2,1)} fusion(bf16[2048,3,8,48]{0,3,2,1:T(8,128)(2,1)} %bitcast.79, f32[8,48]{1,0:T(8,128)S(1)} %fusion.68, f32[8,48,48]{2,1,0:T(8,128)S(1)} %copy-done.8, f32[8,48]{1,0:T(8,128)S(1)} %sqrt.13, f32[8,48]{1,0:T(8,128)S(1)} %sqrt.12, f32[8]{0:T(128)S(1)} %copy-done.11), kind=kOutput, calls=%fused_computation.41 | convolution fusion | flops 76394928 | bytes 3224096 | tf_op jit(solution)/shard_map/nhj,hij->nhi/dot_general | solution.py:28
  110.8 3.9 %fusion.19 = bf16[2048,384]{1,0:T(8,128)(2,1)} fusion(bf16[2048,384]{1,0:T(8,128)(2,1)S(1)} %copy-done.1, bf16[2048,384]{0,1:T(8,128)(2,1)} %bitcast.84, bf16[384,384]{1,0:T(8,128)(2,1)S(1)} %copy-done.9), kind=kOutput, calls=%fused_computation.28 | convolution fusion | flops 606339072 | bytes 5013504 | tf_op jit(solution)/shard_map/dot_general | solution.py:48
  114.7 0.0 copy-done.7
  114.7 3.8 %fusion.67 = (f32[384]{0:T(512)S(1)}, f32[2048]{0:T(1024)S(1)}, f32[2048,384]{1,0:T(8,128)S(1)}) fusion(f32[384]{0:T(512)S(1)} %copy-done.10, f32[2048]{0:T(1024)S(1)} %broadcast_multiply_fusion, bf16[2048,384]{1,0:T(8,128)(2,1)S(1)} %copy-done.1, bf16[2048,1152]{0,1:T(8,128)(2,1)S(1)} %bitcast.82, bf16[384,1152]{1,0:T(8,128)(2,1)S(1)} %copy-done), kind=kOutput, calls=%fused_computation.97 | convolution fusion | flops 1816655488 | bytes 10341376 | tf_op jit(solution)/shard_map/nk,ck->nc/dot_general | solution.py:70
  118.5 1.6 %copy-done.2 = f32[2048,384]{1,0:T(8,128)} copy-done((f32[2048,384]{1,0:T(8,128)}, f32[2048,384]{1,0:T(8,128)S(1)}, u32[]{:S(2)}) %copy-start.2) | copy-done | bytes 3145752
  120.2 1.6 %fusion.12 = (f32[384]{0:T(512)S(1)}, f32[2048]{0:T(1024)S(1)}) fusion(f32[2048,384]{1,0:T(8,128)S(1)} %get-tuple-element.32, bf16[2048,384]{1,0:T(8,128)(2,1)S(1)} %copy-done.1, f32[2048]{0:T(1024)S(1)} %fusion.50, f32[2048]{0:T(1024)S(1)} %broadcast_multiply_fusion, f32[2048]{0:T(1024)S(1)} %multiply_multiply_fusion.1, f32[384]{0:T(512)S(1)} %copy-done.10), kind=kLoop, calls=%fused_computation.21 | loop fusion | flops 8648320 | bytes 4754432 | tf_op jit(solution)/shard_map/transpose(jvp())/reduce_sum | solution.py:11
  121.8 6.8 %all-reduce = (f32[384]{0:T(512)}, f32[384]{0:T(512)}) all-reduce(f32[384]{0:T(512)S(1)} %get-tuple-element.15, f32[384]{0:T(512)S(1)} %get-tuple-element.19), channel_id=1, replica_groups=mesh['dp'=2,'sp'=4] {'sp'}, use_global_device_ids=true, to_apply=%region_20.0 | all-reduce | flops 768 | bytes 6144 | tf_op jit(solution)/shard_map/psum | solution.py:72
  128.6 5.0 %add_convert_fusion = bf16[2048,384]{1,0:T(8,128)(2,1)} fusion(bf16[2048,384]{1,0:T(8,128)(2,1)} %param.8, f32[2048]{0:T(1024)S(1)} %negate_multiply_fusion, f32[2048]{0:T(1024)S(1)} %multiply_multiply_fusion.1, f32[2048]{0:T(1024)S(1)} %broadcast_multiply_fusion, bf16[2048,384]{1,0:T(8,128)(2,1)S(1)} %copy-done.1, f32[2048]{0:T(1024)S(1)} %fusion.50, ...), kind=kLoop, calls=%fused_computation.37 | loop fusion | flops 8650752 | bytes 7898624 | tf_op jit(solution)/shard_map/convert_element_type | solution.py:73
  133.6 1.9 %reduce-scatter.3.cloned.1.call-done = f32[96,1152]{1,0:T(8,128)} async-done(((f32[384,1152]{1,0:T(8,128)}), f32[96,1152]{1,0:T(8,128)}) %reduce-scatter.3.cloned.1.call-update) | async-done | bytes 442384 | tf_op jit(solution)/shard_map/reduce_scatter | solution.py:69
  (16 shorter events, 0.1 us)
Async XLA Ops:
  7.2 4.2 %copy-start = (bf16[384,1152]{1,0:T(8,128)(2,1)S(1)}, bf16[384,1152]{1,0:T(8,128)(2,1)}, u32[]{:S(2)}) copy-start(bf16[384,1152]{1,0:T(8,128)(2,1)} %param.11) | copy-start | bytes 2654212
  7.2 4.2 %copy-start.1 = (bf16[2048,384]{1,0:T(8,128)(2,1)S(1)}, bf16[2048,384]{1,0:T(8,128)(2,1)}, u32[]{:S(2)}) copy-start(bf16[2048,384]{1,0:T(8,128)(2,1)} %param.7) | copy-start | bytes 4718596
  7.2 4.2 %copy-start.10 = (f32[384]{0:T(512)S(1)}, f32[384]{0:T(512)}, u32[]{:S(2)}) copy-start(f32[384]{0:T(512)} %param.9) | copy-start | bytes 4612
  7.2 4.2 %copy-start.12 = (f32[384]{0:T(512)S(1)}, f32[384]{0:T(512)}, u32[]{:S(2)}) copy-start(f32[384]{0:T(512)} %param.10) | copy-start | bytes 4612
  7.2 40.4 %all-reduce.5.cloned.1.call-start = ((), (), s32[]{:S(2)}) async-start(), calls=%async_computation.2 | async-start | bytes 393216 | tf_op jit(solution)/shard_map/psum | solution.py:45
  14.8 2.1 %copy-start.4 = (bf16[2048,1152]{0,1:T(8,128)(2,1)}, bf16[2048,1152]{0,1:T(8,128)(2,1)S(1)}, u32[]{:S(2)}) copy-start(bf16[2048,1152]{0,1:T(8,128)(2,1)S(1)} %convolution_convert_fusion.1) | copy-start | bytes 14155780
  14.8 3.4 %copy-start.9 = (bf16[384,384]{1,0:T(8,128)(2,1)S(1)}, bf16[384,384]{1,0:T(8,128)(2,1)}, u32[]{:S(2)}) copy-start(bf16[384,384]{1,0:T(8,128)(2,1)} %param.12) | copy-start | bytes 884740
  18.2 71.3 %all-reduce.7.cloned.1.call-start = ((), (), s32[]{:S(2)}) async-start(), calls=%async_computation.3 | async-start | bytes 393216 | tf_op jit(solution)/shard_map/psum | solution.py:61
  18.2 3.7 %copy-start.5 = (bf16[2048,1152]{0,1:T(8,128)(2,1)S(1)}, bf16[2048,1152]{0,1:T(8,128)(2,1)}, u32[]{:S(2)}) copy-start(bf16[2048,1152]{0,1:T(8,128)(2,1)} %copy-done.4) | copy-start | bytes 14155780
  22.0 26.8 %copy-start.11 = (f32[8]{0:T(128)S(1)}, f32[8]{0:T(128)}, u32[]{:S(2)}) copy-start(f32[8]{0:T(128)} %param.13) | copy-start | bytes 100
  47.6 1.2 copy-start.8
  62.9 70.7 %reduce-scatter.5.cloned.1.call-start = ((), (), s32[]{:S(2)}) async-start(), calls=%async_computation.5 | async-start | bytes 737280 | tf_op jit(solution)/shard_map/reduce_scatter | solution.py:57
  70.8 64.7 %reduce-scatter.3.cloned.1.call-start = ((), (), s32[]{:S(2)}) async-start(), calls=%async_computation.4 | async-start | bytes 2211840 | tf_op jit(solution)/shard_map/reduce_scatter | solution.py:69
  95.5 2.8 %copy-start.3 = (bf16[2048,1,8,48]{0,3,2,1:T(8,128)(2,1)S(1)}, bf16[2048,1,8,48]{0,3,2,1:T(8,128)(2,1)}, u32[]{:S(2)}) copy-start(bf16[2048,1,8,48]{0,3,2,1:T(8,128)(2,1)} %fusion.24) | copy-start | bytes 4718596
  98.9 2.2 %copy-start.6 = (bf16[2048,3,8,48]{0,3,2,1:T(8,128)(2,1)}, bf16[2048,3,8,48]{0,3,2,1:T(8,128)(2,1)S(1)}, u32[]{:S(2)}) copy-start(bf16[2048,3,8,48]{0,3,2,1:T(8,128)(2,1)S(1)} %pad_maximum_fusion) | copy-start | bytes 14155780
  110.8 3.9 %copy-start.7 = (bf16[2048,3,8,48]{0,3,2,1:T(8,128)(2,1)S(1)}, bf16[2048,3,8,48]{0,3,2,1:T(8,128)(2,1)}, u32[]{:S(2)}) copy-start(bf16[2048,3,8,48]{0,3,2,1:T(8,128)(2,1)} %copy-done.6) | copy-start | bytes 14155780
  118.5 1.7 %copy-start.2 = (f32[2048,384]{1,0:T(8,128)}, f32[2048,384]{1,0:T(8,128)S(1)}, u32[]{:S(2)}) copy-start(f32[2048,384]{1,0:T(8,128)S(1)} %get-tuple-element.32) | copy-start | bytes 9437188
Sparse Core Ops, SparseCore 0:
  18.3 29.2 all-reduce.4
  63.0 26.4 all-reduce.6
  92.5 16.3 reduce-scatter.4
  111.9 23.6 reduce-scatter.2
where the time goes:
time: 142 us
  matrix products  49.8 us (35%)
  waiting for transfers between devices  36.3 us (26%)
  other arithmetic  19.8 us (14%)
  blocking collectives  15.9 us (11%)
  between operations  14.1 us (10%)
  local copies, waits for them, and re-layouts  5.98 us (4%)
    psum x1, waiting for transfers between devices, local_step(): d_probs = lax.psum(probs_part, 'sp')  18.4 us
    psum x1, waiting for transfers between devices, local_step(): gram_sum, q_sq, k_sq = lax.psum((gram_part, qsq_part, ksq_part), 'sp')  15.9 us
    psum x1, blocking collectives, local_step(): gram_sum, q_sq, k_sq = lax.psum((gram_part, qsq_part, ksq_part), 'sp')  9.07 us
    dot_general x2, matrix products, project(): jnp.dot(normed, w_qkv, preferred_element_type=jnp.float32)  8.22 us
    dot_general x2, matrix products, apply_attn(): jnp.einsum('nhj,hij->nhi', v_heads, attn_weights, preferred_element_type=...  8.07 us
    psum x1, blocking collectives, local_step(): grad_gain, grad_bias = lax.psum((gain_part, bias_part), 'sp')  6.82 us
    unnamed x26, local copies, waits for them, and re-layouts  5.96 us
    convert_element_type x1, other arithmetic, local_step(): grad_tokens = (dy_loc.astype(jnp.float32) + d_x).astype(jnp.bfloat16)  5 us
  transfers between devices with their start and end apart: 4, of which 3 were waited for; matrix products, arithmetic and copies ran while one was open for 32% of the time, Pallas kernels for 0%

commit v1 on v0

v1 whole, which is shorter than its diff:
```python
import functools

import jax
import jax.numpy as jnp
from jax import lax
from jax.experimental import pallas as pl
from jax.experimental.pallas import tpu as pltpu
from jax.sharding import PartitionSpec as P

F32, BF16 = jnp.float32, jnp.bfloat16
MESH = pl.DeviceIdType.MESH
BM = 512


def dot_nn(a, b):
    return lax.dot_general(a, b, (((1,), (0,)), ((), ())), preferred_element_type=F32)


def dot_nt(a, b):
    return lax.dot_general(a, b, (((1,), (1,)), ((), ())), preferred_element_type=F32)


def dot_tn(a, b):
    return lax.dot_general(a, b, (((0,), (0,)), ((), ())), preferred_element_type=F32)


def kernel(num_heads, num_sp,
           x_hbm, dy_hbm, gain_ref, bias_ref, wqkv_hbm, wout_hbm, temp_ref,
           out_hbm, gtok_hbm, gwqkv_ref, gwout_ref, ggain_ref, gbias_ref, gtemp_ref,
           x_v, dy_v, wqkv, wout, u_v, ut_v, xhat, rstd, q_v, k_v, v_v, do_v, o_v, dqkv, out_st, gt_st,
           acc, abd, gbd, g_own, g_rx1, g_sum, g_rx2, d_own, d_rx1, d_sum, d_rx2,
           gw, w_rx1, w_sum, w_rx2, gb,
           in_sem, out_sem, gs, gr, ws, wr, bs, br):
    rows_n, dim = x_v.shape
    hd = dim // num_heads
    nb = rows_n // BM
    wrows = dim // num_sp

    me = lax.axis_index('sp')
    partner = me + 1 - 2 * lax.rem(me, 2)
    peer = lax.rem(me + 2, 4)
    diag = lax.rem(partner + 2, 4)

    barrier = pltpu.get_barrier_semaphore()
    for other in (partner, peer, diag):
        pl.semaphore_signal(barrier, inc=1, device_id={'sp': other}, device_id_type=MESH)

    def block(i):
        return pl.ds(pl.multiple_of(i * BM, BM), BM)

    def x_copy(i):
        return pltpu.make_async_copy(x_hbm.at[block(i)], x_v.at[block(i)], in_sem.at[i])

    def dy_copy(i):
        return pltpu.make_async_copy(dy_hbm.at[block(i)], dy_v.at[block(i)], in_sem.at[nb + i])

    wq_copy = pltpu.make_async_copy(wqkv_hbm, wqkv, in_sem.at[2 * nb])
    wo_copy = pltpu.make_async_copy(wout_hbm, wout, in_sem.at[2 * nb + 1])
    x_copy(0).start()
    wq_copy.start()
    for i in range(1, nb):
        x_copy(i).start()
    wo_copy.start()
    for i in range(nb):
        dy_copy(i).start()

    lane = lax.broadcasted_iota(jnp.int32, (hd, dim), 1)
    row = lax.broadcasted_iota(jnp.int32, (hd, dim), 0)
    head_mask = [(lane >= h * hd) & (lane < (h + 1) * hd) for h in range(num_heads)]

    def fold(full_ref):
        total = jnp.zeros((hd, dim), F32)
        for h in range(num_heads):
            total = jnp.where(head_mask[h], full_ref[h * hd:(h + 1) * hd, :], total)
        return total

    def expand(ref, compact):
        for h in range(num_heads):
            ref[h * hd:(h + 1) * hd, :] = jnp.where(head_mask[h], compact, 0.0).astype(BF16)

    def send(src, dst, ssem, rsem, dev):
        return pltpu.make_async_remote_copy(src_ref=src, dst_ref=dst, send_sem=ssem, recv_sem=rsem,
                                            device_id={'sp': dev}, device_id_type=MESH)

    gain = gain_ref[...].reshape(1, dim)
    bias = bias_ref[...].reshape(1, dim)
    inv_d = 1.0 / dim

    wq_copy.wait()

    acc[...] = jnp.zeros_like(acc)

    def p1(i, carry):
        sq, sk = carry
        r = block(i)
        x_copy(i).wait()
        xf = x_v[r, :].astype(F32)
        cen = xf - jnp.sum(xf, axis=-1, keepdims=True) * inv_d
        var = jnp.sum(cen * cen, axis=-1, keepdims=True) * inv_d
        rs = lax.rsqrt(var + 1e-6)
        xh = cen * rs
        xhat[r, :] = xh
        rstd[r, :] = jnp.broadcast_to(rs, (BM, 128))
        u = (xh * gain + bias).astype(BF16)
        u_v[r, :] = u
        qk = dot_nn(u, wqkv[:, :2 * dim]).astype(BF16)
        q, k = qk[:, :dim], qk[:, dim:]
        q_v[r, :] = q
        k_v[r, :] = k
        acc[...] += dot_tn(k, q)
        qf, kf = q.astype(F32), k.astype(F32)
        sq = sq + jnp.sum((qf * qf).reshape(BM // 8, 8, dim), axis=0)
        sk = sk + jnp.sum((kf * kf).reshape(BM // 8, 8, dim), axis=0)
        return sq, sk

    zero8 = jnp.zeros((8, dim), F32)
    sq, sk = lax.fori_loop(0, nb, p1, (zero8, zero8))
    g_own[:hd, :] = fold(acc)
    row8 = lax.broadcasted_iota(jnp.int32, (8, dim), 0)
    g_own[hd:hd + 8, :] = jnp.where(row8 == 0, jnp.sum(sq, axis=0, keepdims=True),
                                    jnp.where(row8 == 1, jnp.sum(sk, axis=0, keepdims=True), 0.0))

    pl.semaphore_wait(barrier, 3)
    g1 = send(g_own, g_rx1, gs.at[0], gr.at[0], partner)
    g1.start()

    acc[...] = jnp.zeros_like(acc)
    wo_copy.wait()

    def p2(i, carry):
        r = block(i)
        dy_copy(i).wait()
        u = u_v[r, :]
        v = dot_nn(u, wqkv[:, 2 * dim:]).astype(BF16)
        v_v[r, :] = v
        do = dot_nt(dy_v[r, :], wout[...]).astype(BF16)
        do_v[r, :] = do
        acc[...] += dot_tn(v, do)
        ut_v[:, r] = u.T
        return carry

    lax.fori_loop(0, nb // 2, p2, 0)
    g1.wait()
    g_sum[...] = g_own[...] + g_rx1[...]
    g2 = send(g_sum, g_rx2, gs.at[1], gr.at[1], peer)
    g2.start()
    lax.fori_loop(nb // 2, nb, p2, 0)

    d_own[...] = fold(acc)
    d1 = send(d_own, d_rx1, gs.at[2], gr.at[2], partner)
    d1.start()
    d1.wait()
    d_sum[...] = d_own[...] + d_rx1[...]
    d2 = send(d_sum, d_rx2, gs.at[3], gr.at[3], peer)
    d2.start()

    g2.wait()
    tot = g_sum[...] + g_rx2[...]
    gram = tot[:hd, :]
    sq_row = tot[hd:hd + 1, :]
    sk_row = tot[hd + 1:hd + 2, :]
    sk_full = jnp.zeros((hd, dim), F32)
    for h in range(num_heads):
        col = jnp.sum(jnp.where(lane == row + h * hd, sk_row, 0.0), axis=1, keepdims=True)
        sk_full = jnp.where(head_mask[h], col, sk_full)
    tau = jnp.zeros((1, dim), F32)
    for h in range(num_heads):
        tau = jnp.where(head_mask[h][:1, :], temp_ref[h], tau)
    denom = jnp.sqrt(sq_row) * jnp.sqrt(sk_full)
    cos = gram / denom
    s = tau * cos
    e = jnp.exp(s - jnp.max(s, axis=0, keepdims=True))
    prob = e / jnp.sum(e, axis=0, keepdims=True)
    expand(abd, prob)

    def pair_send(c, part):
        rows = pl.ds(pl.multiple_of((partner if part else diag) * wrows, 8), wrows)
        return send(gw.at[c, rows, :], w_rx1.at[c, part], ws.at[3 * c + part], wr.at[3 * c + part], partner)

    def cross_send(c):
        return send(w_sum.at[c], w_rx2.at[c], ws.at[3 * c + 2], wr.at[3 * c + 2], peer)

    def pair_start(c):
        pair_send(c, 0).start()
        pair_send(c, 1).start()

    def cross_start(c):
        pair_send(c, 0).wait()
        w_sum[c] = gw[c, pl.ds(pl.multiple_of(peer * wrows, 8), wrows), :] + w_rx1[c, 0]
        cross_send(c).start()

    def p3(i, carry):
        r = block(i)
        dqkv[r, 2 * dim:] = dot_nt(do_v[r, :], abd[...]).astype(BF16)
        return carry

    lax.fori_loop(0, nb, p3, 0)
    gw[2] = dot_nn(ut_v[...], dqkv[:, 2 * dim:])
    pair_start(2)

    def p4(i, carry):
        r = block(i)
        o_v[r, :] = dot_nn(v_v[r, :], abd[...]).astype(BF16)
        return carry

    lax.fori_loop(0, nb, p4, 0)
    cross_start(2)
    gw[3] = dot_tn(o_v[...], dy_v[...])
    pair_start(3)

    d2.wait()
    da = d_sum[...] + d_rx2[...]
    ds = prob * (da - jnp.sum(prob * da, axis=0, keepdims=True))
    dcos = tau * ds
    t_row = jnp.sum(ds * cos, axis=0, keepdims=True)
    lane_t = lax.broadcasted_iota(jnp.int32, (1, num_heads), 1)
    g_temp = jnp.zeros((1, num_heads), F32)
    for h in range(num_heads):
        val = jnp.sum(jnp.where(head_mask[h][:1, :], t_row, 0.0), axis=1, keepdims=True)
        g_temp = jnp.where(lane_t == h, val, g_temp)
    gtemp_ref[...] = g_temp
    expand(gbd, dcos / denom)
    z = dcos * cos
    dsq2 = -jnp.sum(z, axis=0, keepdims=True) / sq_row
    sk_grad = jnp.zeros((hd, dim), F32)
    for h in range(num_heads):
        col = jnp.sum(jnp.where(head_mask[h], z, 0.0), axis=1, keepdims=True)
        sk_grad = jnp.where(lane == row + h * hd, col, sk_grad)
    dsk2 = -jnp.sum(sk_grad, axis=0, keepdims=True) / sk_row

    def p5(i, carry):
        r = block(i)
        dqkv[r, :dim] = (dot_nn(k_v[r, :], gbd[...]) + q_v[r, :].astype(F32) * dsq2).astype(BF16)
        return carry

    lax.fori_loop(0, nb, p5, 0)
    cross_start(3)
    gw[0] = dot_nn(ut_v[...], dqkv[:, :dim])
    pair_start(0)

    def p6(i, carry):
        r = block(i)
        dqkv[r, dim:2 * dim] = (dot_nt(q_v[r, :], gbd[...]) + k_v[r, :].astype(F32) * dsk2).astype(BF16)
        return carry

    lax.fori_loop(0, nb, p6, 0)
    cross_start(0)
    gw[1] = dot_nn(ut_v[...], dqkv[:, dim:2 * dim])
    pair_start(1)

    def out_copy(i):
        return pltpu.make_async_copy(out_st.at[block(i)], out_hbm.at[block(i)], out_sem.at[i])

    def gt_copy(i):
        return pltpu.make_async_copy(gt_st.at[block(i)], gtok_hbm.at[block(i)], out_sem.at[nb + i])

    def p7(i, carry):
        r = block(i)
        y = dot_nn(o_v[r, :], wout[...])
        out_st[r, :] = (x_v[r, :].astype(F32) + y).astype(BF16)
        out_copy(i).start()
        return carry

    lax.fori_loop(0, nb, p7, 0)
    cross_start(1)

    def p8(i, carry):
        gg, gbi = carry
        r = block(i)
        du = dot_nt(dqkv[r, :], wqkv[...])
        xh = xhat[r, :]
        dux = du * xh
        gg = gg + jnp.sum(dux.reshape(BM // 8, 8, dim), axis=0)
        gbi = gbi + jnp.sum(du.reshape(BM // 8, 8, dim), axis=0)
        m1 = jnp.sum(du * gain, axis=-1, keepdims=True) * inv_d
        m2 = jnp.sum(dux * gain, axis=-1, keepdims=True) * inv_d
        dx = (du * gain - m1 - xh * m2) * rstd[r, :1]
        gt_st[r, :] = (dy_v[r, :].astype(F32) + dx).astype(BF16)
        gt_copy(i).start()
        return gg, gbi

    gg, gbi = lax.fori_loop(0, nb, p8, (zero8, zero8))
    gb[me] = jnp.where(row8 == 0, jnp.sum(gg, axis=0, keepdims=True),
                       jnp.where(row8 == 1, jnp.sum(gbi, axis=0, keepdims=True), 0.0))
    gbc = [send(gb.at[me], gb.at[me], bs.at[n], br.at[n], other) for n, other in enumerate((partner, peer, diag))]
    for c in gbc:
        c.start()

    mine = pl.ds(pl.multiple_of(me * wrows, 8), wrows)
    for c in (2, 3, 0, 1):
        pair_send(c, 1).wait()
        cross_send(c).wait()
        total = gw[c, mine, :] + w_rx1[c, 1] + w_rx2[c]
        if c == 3:
            gwout_ref[...] = total
        else:
            gwqkv_ref[:, c * dim:(c + 1) * dim] = total
    for c in gbc:
        c.wait()
    gsum = (gb[0] + gb[1]) + (gb[2] + gb[3])
    ggain_ref[...] = gsum[0:1, :]
    gbias_ref[...] = gsum[1:2, :]

    def drain(i, carry):
        out_copy(i).wait()
        gt_copy(i).wait()
        return carry

    lax.fori_loop(0, nb, drain, 0)


def solution(mesh):
    row_spec = P(('dp', 'sp'), None)
    part_spec = P('dp')
    full_spec = P()
    num_sp = mesh.shape['sp']

    def local_step(x, dy, gain, bias, w_qkv, w_out, temperature):
        n, d = x.shape
        h = temperature.shape[0]
        hd = d // h
        wrows = d // num_sp
        nb = n // BM
        vmem = pl.BlockSpec(memory_space=pltpu.VMEM)
        smem = pl.BlockSpec(memory_space=pltpu.SMEM)
        hbm = pl.BlockSpec(memory_space=pl.ANY)
        tok = pltpu.VMEM((n, d), BF16)
        sds = jax.ShapeDtypeStruct
        dma = pltpu.SemaphoreType.DMA
        outs = pl.pallas_call(
            functools.partial(kernel, h, num_sp),
            name='xca',
            out_shape=(sds((n, d), BF16), sds((n, d), BF16), sds((wrows, 3 * d), F32), sds((wrows, d), F32),
                       sds((1, d), F32), sds((1, d), F32), sds((1, h), F32)),
            in_specs=[hbm, hbm, vmem, vmem, hbm, hbm, smem],
            out_specs=(hbm, hbm, vmem, vmem, vmem, vmem, vmem),
            scratch_shapes=[
                tok, tok, pltpu.VMEM((d, 3 * d), BF16), pltpu.VMEM((d, d), BF16), tok, pltpu.VMEM((d, n), BF16),
                pltpu.VMEM((n, d), F32), pltpu.VMEM((n, 128), F32), tok, tok, tok, tok, tok,
                pltpu.VMEM((n, 3 * d), BF16), tok, tok,
                pltpu.VMEM((d, d), F32), pltpu.VMEM((d, d), BF16), pltpu.VMEM((d, d), BF16),
                pltpu.VMEM((hd + 8, d), F32), pltpu.VMEM((hd + 8, d), F32), pltpu.VMEM((hd + 8, d), F32),
                pltpu.VMEM((hd + 8, d), F32),
                pltpu.VMEM((hd, d), F32), pltpu.VMEM((hd, d), F32), pltpu.VMEM((hd, d), F32), pltpu.VMEM((hd, d), F32),
                pltpu.VMEM((4, d, d), F32), pltpu.VMEM((4, 2, wrows, d), F32), pltpu.VMEM((4, wrows, d), F32),
                pltpu.VMEM((4, wrows, d), F32), pltpu.VMEM((4, 8, d), F32),
                dma((2 * nb + 2,)), dma((2 * nb,)), dma((4,)), dma((4,)), dma((12,)), dma((12,)), dma((3,)), dma((3,)),
            ],
            compiler_params=pltpu.CompilerParams(collective_id=0, has_side_effects=True,
                                                 vmem_limit_bytes=60 * 1024 * 1024),
        )(x, dy, gain, bias, w_qkv, w_out, temperature)
        out, gtok, gwqkv, gwout, ggain, gbias, gtemp = outs
        return out, gtok, gwqkv, gwout, ggain.reshape(d), gbias.reshape(d), gtemp.reshape(h)

    return jax.shard_map(local_step, mesh=mesh,
                         in_specs=(row_spec, row_spec, full_spec, full_spec, full_spec, full_spec, full_spec),
                         out_specs=(row_spec, row_spec, row_spec, row_spec, part_spec, part_spec, part_spec),
                         check_vma=False)
```

time: 142 us -> 44.8 us (0.32)
  matrix products: 49.8 us -> 0 us
  waiting for transfers between devices: 36.3 us -> 0 us
  Pallas kernels: 0 us -> 35.4 us
  other arithmetic: 19.8 us -> 2.54 us
  blocking collectives: 15.9 us -> 0 us
  between operations: 14.1 us -> 0.65 us
    dot_general x14 -> x0, matrix products: 49.8 us -> none  [the longest x2 8.22 us: project(): jnp.dot(normed, w_qkv, preferred_element_type=jnp.float32)]
    pallas_call x0 -> x1, Pallas kernels: none -> 35.4 us  [local_step(): pl.pallas_call(functools.partial(kernel, h, num_sp), name='xca', out_shap...]
    psum x2 -> x0, waiting for transfers between devices: 34.3 us -> none  [the longest x1 18.4 us: local_step(): d_probs = lax.psum(probs_part, 'sp')]
    psum x2 -> x0, blocking collectives: 15.9 us -> none  [the longest x1 9.07 us: local_step(): gram_sum, q_sq, k_sq = lax.psum((gram_part, qsq_part, ksq_part), 'sp')]
    reduce_sum x7 -> x0, other arithmetic: 8.8 us -> none  [the longest x2 3.02 us: layer_norm(): row_var = jnp.mean(centered * centered, axis=-1, keepdims=True)]
    convert_element_type x1 -> x0, other arithmetic: 5 us -> none  [local_step(): grad_tokens = (dy_loc.astype(jnp.float32) + d_x).astype(jnp.bfloat16)]
    sub x2 -> x0, other arithmetic: 3.51 us -> none  [attn_probs(): return jax.nn.softmax(value_a11[..., None, None] * cosine, axis=-1)]
    pallas_call x0 -> x2, other arithmetic: none -> 2.54 us  [local_step(): pl.pallas_call(functools.partial(kernel, h, num_sp), name='xca', out_shap...]
  transfers between devices with their start and end apart: 4 -> 0, of which waited for: 3 -> 0; matrix products, arithmetic and copies ran while one was open for 32% -> 0% of each run, Pallas kernels for 0% -> 0%
where the time goes in v1:
time: 44.8 us; the launch traced here: 44.6 us
  Pallas kernels  35.4 us (79%)
  local copies, waits for them, and re-layouts  6.04 us (13%)
  other arithmetic  2.54 us (6%)
  between operations  0.65 us (1%)
    pallas_call x1, Pallas kernels, local_step(): pl.pallas_call(functools.partial(kernel, h, num_sp), name='xca', out_shap...  35.4 us
    unnamed x13, local copies, waits for them, and re-layouts  6.04 us
    pallas_call x2, other arithmetic, local_step(): pl.pallas_call(functools.partial(kernel, h, num_sp), name='xca', out_shap...  2.54 us

profile of v1, /device:TPU:0, one launch (start us, length us, event | category | flops | bytes accessed | tf_op | source)
XLA Modules:
  0.0 44.6 jit_solution(17326034177641265626)
XLA Ops:
  0.6 35.4 %xca.1 = (bf16[2048,384]{1,0:T(8,128)(2,1)}, bf16[2048,384]{1,0:T(8,128)(2,1)}, f32[96,1152]{1,0:T(8,128)}, f32[96,384]{1,0:T(8,128)}, f32[1,384]{1,0:T(1,128)}, /*index=5*/f32[1,384]{1,0:T(1,128)}, f32[1,8]{1,0:T(1,128)}) custom-call(bf16[2048,384]{1,0:T(8,128)(2,1)} %x_hbm.1, bf16[2048,384]{1,0:T(8,128)(2,1)} %dy_hbm.1, f32[384]{0:T(512)} %gain_ref.1, ...), custom_call_target="tpu_custom_call" | custom-call | tf_op jit(solution)/shard_map/xca/pallas_call | solution.py:330
  36.0 1.3 %reduce = f32[384]{0:T(512)} reduce(f32[1,384]{1,0:T(1,128)} %get-tuple-element.18, f32[]{:T(128)} %constant), dimensions={0}, to_apply=%get-tuple-element.18.reduce_sub_computation | reduce | bytes 3076 | tf_op jit(solution)/shard_map/xca/pallas_call | solution.py:330
  37.3 1.3 %reduce.1 = f32[384]{0:T(512)} reduce(f32[1,384]{1,0:T(1,128)} %get-tuple-element.19, f32[]{:T(128)} %constant), dimensions={0}, to_apply=%get-tuple-element.19.reduce_sub_computation | reduce | bytes 3076 | tf_op jit(solution)/shard_map/xca/pallas_call | solution.py:330
  38.5 0.0 copy-start
  38.5 2.8 %copy.19 = bf16[2048,384]{1,0:T(8,128)(2,1)} copy(bf16[2048,384]{1,0:T(8,128)(2,1)} %get-tuple-element.28) | data formatting | bytes 3145728
  41.4 0.0 copy-done
  41.4 0.0 copy-start.1
  41.4 0.0 copy-start.2
  41.4 0.0 copy-start.3
  41.4 1.1 %copy.20 = bf16[2048,384]{1,0:T(8,128)(2,1)} copy(bf16[2048,384]{1,0:T(8,128)(2,1)S(1)} %copy-done) | data formatting | bytes 3145728
  42.5 0.1 copy-done.1
  42.6 0.8 %copy.21 = f32[96,1152]{1,0:T(8,128)} copy(f32[96,1152]{1,0:T(8,128)S(1)} %copy-done.1) | data formatting | bytes 884736
  43.4 0.0 copy-done.2
  43.4 0.7 %copy.22 = f32[96,384]{1,0:T(8,128)} copy(f32[96,384]{1,0:T(8,128)S(1)} %copy-done.2) | data formatting | bytes 294912
  44.1 0.0 copy-done.3
  44.1 0.5 %copy.23 = f32[8]{0:T(128)} copy(f32[8]{0:T(128)S(1)} %bitcast.1) | data formatting | bytes 64
Async XLA Ops:
  38.5 2.8 %copy-start = (bf16[2048,384]{1,0:T(8,128)(2,1)S(1)}, bf16[2048,384]{1,0:T(8,128)(2,1)}, u32[]{:S(2)}) copy-start(bf16[2048,384]{1,0:T(8,128)(2,1)} %get-tuple-element.29) | copy-start | bytes 4718596
  41.4 1.3 %copy-start.1 = (f32[96,1152]{1,0:T(8,128)S(1)}, f32[96,1152]{1,0:T(8,128)}, u32[]{:S(2)}) copy-start(f32[96,1152]{1,0:T(8,128)} %get-tuple-element.30) | copy-start | bytes 1327108
  41.4 2.0 %copy-start.2 = (f32[96,384]{1,0:T(8,128)S(1)}, f32[96,384]{1,0:T(8,128)}, u32[]{:S(2)}) copy-start(f32[96,384]{1,0:T(8,128)} %get-tuple-element.31) | copy-start | bytes 442372
  41.4 2.7 %copy-start.3 = (f32[1,8]{1,0:T(1,128)S(1)}, f32[1,8]{1,0:T(1,128)}, u32[]{:S(2)}) copy-start(f32[1,8]{1,0:T(1,128)} %get-tuple-element.20) | copy-start | bytes 100

commit v2 on v1

--- a/solution.py
+++ b/solution.py
@@ -25,12 +25,12 @@
 
 
 def kernel(num_heads, num_sp,
-           x_hbm, dy_hbm, gain_ref, bias_ref, wqkv_hbm, wout_hbm, temp_ref,
-           out_hbm, gtok_hbm, gwqkv_ref, gwout_ref, ggain_ref, gbias_ref, gtemp_ref,
-           x_v, dy_v, wqkv, wout, u_v, ut_v, xhat, rstd, q_v, k_v, v_v, do_v, o_v, dqkv, out_st, gt_st,
+           x_hbm, dy_hbm, gain_hbm, bias_hbm, wqkv_hbm, wout_hbm, temp_hbm,
+           out_st, gt_st, gwqkv_ref, gwout_ref, ggain_ref, gbias_ref, gtemp_ref,
+           gain_ref, bias_ref, temp_ref, x_v, dy_v, wqkv, wout, u_v, ut_v, xhat, rstd, q_v, k_v, v_v, do_v, o_v, dqkv,
            acc, abd, gbd, g_own, g_rx1, g_sum, g_rx2, d_own, d_rx1, d_sum, d_rx2,
            gw, w_rx1, w_sum, w_rx2, gb,
-           in_sem, out_sem, gs, gr, ws, wr, bs, br):
+           in_sem, gs, gr, ws, wr, bs, br):
     rows_n, dim = x_v.shape
     hd = dim // num_heads
     nb = rows_n // BM
@@ -56,7 +56,11 @@
 
     wq_copy = pltpu.make_async_copy(wqkv_hbm, wqkv, in_sem.at[2 * nb])
     wo_copy = pltpu.make_async_copy(wout_hbm, wout, in_sem.at[2 * nb + 1])
+    small = [pltpu.make_async_copy(a, b, in_sem.at[2 * nb + 2 + n]) for n, (a, b) in enumerate(
+        ((gain_hbm, gain_ref), (bias_hbm, bias_ref), (temp_hbm, temp_ref)))]
     x_copy(0).start()
+    for c in small:
+        c.start()
     wq_copy.start()
     for i in range(1, nb):
         x_copy(i).start()
@@ -82,6 +86,8 @@
         return pltpu.make_async_remote_copy(src_ref=src, dst_ref=dst, send_sem=ssem, recv_sem=rsem,
                                             device_id={'sp': dev}, device_id_type=MESH)
 
+    for c in small:
+        c.wait()
     gain = gain_ref[...].reshape(1, dim)
     bias = bias_ref[...].reshape(1, dim)
     inv_d = 1.0 / dim
@@ -114,13 +120,15 @@
         return sq, sk
 
     zero8 = jnp.zeros((8, dim), F32)
-    sq, sk = lax.fori_loop(0, nb, p1, (zero8, zero8))
+    with jax.named_scope('p1'):
+        sq, sk = lax.fori_loop(0, nb, p1, (zero8, zero8))
     g_own[:hd, :] = fold(acc)
     row8 = lax.broadcasted_iota(jnp.int32, (8, dim), 0)
     g_own[hd:hd + 8, :] = jnp.where(row8 == 0, jnp.sum(sq, axis=0, keepdims=True),
                                     jnp.where(row8 == 1, jnp.sum(sk, axis=0, keepdims=True), 0.0))
 
-    pl.semaphore_wait(barrier, 3)
+    with jax.named_scope('barw'):
+        pl.semaphore_wait(barrier, 3)
     g1 = send(g_own, g_rx1, gs.at[0], gr.at[0], partner)
     g1.start()
 
@@ -139,22 +147,27 @@
         ut_v[:, r] = u.T
         return carry
 
-    lax.fori_loop(0, nb // 2, p2, 0)
-    g1.wait()
+    with jax.named_scope('p2a'):
+        lax.fori_loop(0, nb // 2, p2, 0)
+    with jax.named_scope('g1w'):
+        g1.wait()
     g_sum[...] = g_own[...] + g_rx1[...]
     g2 = send(g_sum, g_rx2, gs.at[1], gr.at[1], peer)
     g2.start()
-    lax.fori_loop(nb // 2, nb, p2, 0)
+    with jax.named_scope('p2b'):
+        lax.fori_loop(nb // 2, nb, p2, 0)
 
     d_own[...] = fold(acc)
     d1 = send(d_own, d_rx1, gs.at[2], gr.at[2], partner)
     d1.start()
-    d1.wait()
+    with jax.named_scope('d1w'):
+        d1.wait()
     d_sum[...] = d_own[...] + d_rx1[...]
     d2 = send(d_sum, d_rx2, gs.at[3], gr.at[3], peer)
     d2.start()
 
-    g2.wait()
+    with jax.named_scope('g2w'):
+        g2.wait()
     tot = g_sum[...] + g_rx2[...]
     gram = tot[:hd, :]
     sq_row = tot[hd:hd + 1, :]
@@ -194,8 +207,10 @@
         dqkv[r, 2 * dim:] = dot_nt(do_v[r, :], abd[...]).astype(BF16)
         return carry
 
-    lax.fori_loop(0, nb, p3, 0)
-    gw[2] = dot_nn(ut_v[...], dqkv[:, 2 * dim:])
+    with jax.named_scope('p3'):
+        lax.fori_loop(0, nb, p3, 0)
+    with jax.named_scope('gw2'):
+        gw[2] = dot_nn(ut_v[...], dqkv[:, 2 * dim:])
     pair_start(2)
 
     def p4(i, carry):
@@ -203,12 +218,16 @@
         o_v[r, :] = dot_nn(v_v[r, :], abd[...]).astype(BF16)
         return carry
 
-    lax.fori_loop(0, nb, p4, 0)
-    cross_start(2)
-    gw[3] = dot_tn(o_v[...], dy_v[...])
+    with jax.named_scope('p4'):
+        lax.fori_loop(0, nb, p4, 0)
+    with jax.named_scope('cs2'):
+        cross_start(2)
+    with jax.named_scope('gw3'):
+        gw[3] = dot_tn(o_v[...], dy_v[...])
     pair_start(3)
 
-    d2.wait()
+    with jax.named_scope('d2w'):
+        d2.wait()
     da = d_sum[...] + d_rx2[...]
     ds = prob * (da - jnp.sum(prob * da, axis=0, keepdims=True))
     dcos = tau * ds
@@ -233,9 +252,12 @@
         dqkv[r, :dim] = (dot_nn(k_v[r, :], gbd[...]) + q_v[r, :].astype(F32) * dsq2).astype(BF16)
         return carry
 
-    lax.fori_loop(0, nb, p5, 0)
-    cross_start(3)
-    gw[0] = dot_nn(ut_v[...], dqkv[:, :dim])
+    with jax.named_scope('p5'):
+        lax.fori_loop(0, nb, p5, 0)
+    with jax.named_scope('cs3'):
+        cross_start(3)
+    with jax.named_scope('gw0'):
+        gw[0] = dot_nn(ut_v[...], dqkv[:, :dim])
     pair_start(0)
 
     def p6(i, carry):
@@ -243,26 +265,24 @@
         dqkv[r, dim:2 * dim] = (dot_nt(q_v[r, :], gbd[...]) + k_v[r, :].astype(F32) * dsk2).astype(BF16)
         return carry
 
-    lax.fori_loop(0, nb, p6, 0)
-    cross_start(0)
-    gw[1] = dot_nn(ut_v[...], dqkv[:, dim:2 * dim])
+    with jax.named_scope('p6'):
+        lax.fori_loop(0, nb, p6, 0)
+    with jax.named_scope('cs0'):
+        cross_start(0)
+    with jax.named_scope('gw1'):
+        gw[1] = dot_nn(ut_v[...], dqkv[:, dim:2 * dim])
     pair_start(1)
-
-    def out_copy(i):
-        return pltpu.make_async_copy(out_st.at[block(i)], out_hbm.at[block(i)], out_sem.at[i])
-
-    def gt_copy(i):
-        return pltpu.make_async_copy(gt_st.at[block(i)], gtok_hbm.at[block(i)], out_sem.at[nb + i])
 
     def p7(i, carry):
         r = block(i)
         y = dot_nn(o_v[r, :], wout[...])
         out_st[r, :] = (x_v[r, :].astype(F32) + y).astype(BF16)
-        out_copy(i).start()
-        return carry
-
-    lax.fori_loop(0, nb, p7, 0)
-    cross_start(1)
+        return carry
+
+    with jax.named_scope('p7'):
+        lax.fori_loop(0, nb, p7, 0)
+    with jax.named_scope('cs1'):
+        cross_start(1)
 
     def p8(i, carry):
         gg, gbi = carry
@@ -276,10 +296,10 @@
         m2 = jnp.sum(dux * gain, axis=-1, keepdims=True) * inv_d
         dx = (du * gain - m1 - xh * m2) * rstd[r, :1]
         gt_st[r, :] = (dy_v[r, :].astype(F32) + dx).astype(BF16)
-        gt_copy(i).start()
         return gg, gbi
 
-    gg, gbi = lax.fori_loop(0, nb, p8, (zero8, zero8))
+    with jax.named_scope('p8'):
+        gg, gbi = lax.fori_loop(0, nb, p8, (zero8, zero8))
     gb[me] = jnp.where(row8 == 0, jnp.sum(gg, axis=0, keepdims=True),
                        jnp.where(row8 == 1, jnp.sum(gbi, axis=0, keepdims=True), 0.0))
     gbc = [send(gb.at[me], gb.at[me], bs.at[n], br.at[n], other) for n, other in enumerate((partner, peer, diag))]
@@ -288,25 +308,32 @@
 
     mine = pl.ds(pl.multiple_of(me * wrows, 8), wrows)
     for c in (2, 3, 0, 1):
-        pair_send(c, 1).wait()
-        cross_send(c).wait()
+        with jax.named_scope(f'fin{c}'):
+            pair_send(c, 1).wait()
+            cross_send(c).wait()
         total = gw[c, mine, :] + w_rx1[c, 1] + w_rx2[c]
         if c == 3:
             gwout_ref[...] = total
         else:
             gwqkv_ref[:, c * dim:(c + 1) * dim] = total
-    for c in gbc:
-        c.wait()
+    with jax.named_scope('gbw'):
+        for c in gbc:
+            c.wait()
     gsum = (gb[0] + gb[1]) + (gb[2] + gb[3])
     ggain_ref[...] = gsum[0:1, :]
     gbias_ref[...] = gsum[1:2, :]
 
-    def drain(i, carry):
-        out_copy(i).wait()
-        gt_copy(i).wait()
-        return carry
-
-    lax.fori_loop(0, nb, drain, 0)
+
+def finish(out_v, gt_v, gwqkv_v, gwout_v, ggain_v, gbias_v, gtemp_v,
+           out_hbm, gt_hbm, gwqkv_hbm, gwout_hbm, ggain_ref, gbias_ref, gtemp_ref, sem):
+    pairs = ((out_v, out_hbm), (gt_v, gt_hbm), (gwqkv_v, gwqkv_hbm), (gwout_v, gwout_hbm))
+    copies = [pltpu.make_async_copy(src, dst, sem.at[n]) for n, (src, dst) in enumerate(pairs)]
+    for c in copies:
+        c.start()
+    for src, dst in ((ggain_v, ggain_ref), (gbias_v, gbias_ref), (gtemp_v, gtemp_ref)):
+        dst[...] = src[...].reshape(dst.shape)
+    for c in copies:
+        c.wait()
 
 
 def solution(mesh):
@@ -322,35 +349,44 @@
         wrows = d // num_sp
         nb = n // BM
         vmem = pl.BlockSpec(memory_space=pltpu.VMEM)
-        smem = pl.BlockSpec(memory_space=pltpu.SMEM)
-        hbm = pl.BlockSpec(memory_space=pl.ANY)
+        hbm = pl.BlockSpec(memory_space=pltpu.HBM)
         tok = pltpu.VMEM((n, d), BF16)
         sds = jax.ShapeDtypeStruct
         dma = pltpu.SemaphoreType.DMA
+        in_hbm = functools.partial(pltpu.with_memory_space_constraint, memory_space=pltpu.HBM)
         outs = pl.pallas_call(
             functools.partial(kernel, h, num_sp),
             name='xca',
-            out_shape=(sds((n, d), BF16), sds((n, d), BF16), sds((wrows, 3 * d), F32), sds((wrows, d), F32),
-                       sds((1, d), F32), sds((1, d), F32), sds((1, h), F32)),
-            in_specs=[hbm, hbm, vmem, vmem, hbm, hbm, smem],
-            out_specs=(hbm, hbm, vmem, vmem, vmem, vmem, vmem),
+            out_shape=(pltpu.VMEM((n, d), BF16), pltpu.VMEM((n, d), BF16), pltpu.VMEM((wrows, 3 * d), F32),
+                       pltpu.VMEM((wrows, d), F32), pltpu.VMEM((1, d), F32), pltpu.VMEM((1, d), F32),
+                       pltpu.VMEM((1, h), F32)),
+            in_specs=[hbm] * 7,
+            out_specs=(vmem,) * 7,
             scratch_shapes=[
-                tok, tok, pltpu.VMEM((d, 3 * d), BF16), pltpu.VMEM((d, d), BF16), tok, pltpu.VMEM((d, n), BF16),
+                pltpu.VMEM((d,), F32), pltpu.VMEM((d,), F32), pltpu.SMEM((h,), F32), tok, tok, pltpu.VMEM((d, 3 * d), BF16), pltpu.VMEM((d, d), BF16), tok, pltpu.VMEM((d, n), BF16),
                 pltpu.VMEM((n, d), F32), pltpu.VMEM((n, 128), F32), tok, tok, tok, tok, tok,
-                pltpu.VMEM((n, 3 * d), BF16), tok, tok,
+                pltpu.VMEM((n, 3 * d), BF16),
                 pltpu.VMEM((d, d), F32), pltpu.VMEM((d, d), BF16), pltpu.VMEM((d, d), BF16),
                 pltpu.VMEM((hd + 8, d), F32), pltpu.VMEM((hd + 8, d), F32), pltpu.VMEM((hd + 8, d), F32),
                 pltpu.VMEM((hd + 8, d), F32),
                 pltpu.VMEM((hd, d), F32), pltpu.VMEM((hd, d), F32), pltpu.VMEM((hd, d), F32), pltpu.VMEM((hd, d), F32),
                 pltpu.VMEM((4, d, d), F32), pltpu.VMEM((4, 2, wrows, d), F32), pltpu.VMEM((4, wrows, d), F32),
                 pltpu.VMEM((4, wrows, d), F32), pltpu.VMEM((4, 8, d), F32),
-                dma((2 * nb + 2,)), dma((2 * nb,)), dma((4,)), dma((4,)), dma((12,)), dma((12,)), dma((3,)), dma((3,)),
+                dma((2 * nb + 5,)), dma((4,)), dma((4,)), dma((12,)), dma((12,)), dma((3,)), dma((3,)),
             ],
             compiler_params=pltpu.CompilerParams(collective_id=0, has_side_effects=True,
-                                                 vmem_limit_bytes=60 * 1024 * 1024),
-        )(x, dy, gain, bias, w_qkv, w_out, temperature)
-        out, gtok, gwqkv, gwout, ggain, gbias, gtemp = outs
-        return out, gtok, gwqkv, gwout, ggain.reshape(d), gbias.reshape(d), gtemp.reshape(h)
+                                                 vmem_limit_bytes=40 * 1024 * 1024),
+        )(*map(in_hbm, (x, dy, gain, bias, w_qkv, w_out, temperature)))
+        return pl.pallas_call(
+            finish,
+            name='finish',
+            out_shape=(sds((n, d), BF16), sds((n, d), BF16), sds((wrows, 3 * d), F32), sds((wrows, d), F32),
+                       sds((d,), F32), sds((d,), F32), sds((h,), F32)),
+            in_specs=[vmem] * 7,
+            out_specs=(hbm, hbm, hbm, hbm, vmem, vmem, vmem),
+            scratch_shapes=[dma((4,))],
+            compiler_params=pltpu.CompilerParams(vmem_limit_bytes=8 * 1024 * 1024),
+        )(*outs)
 
     return jax.shard_map(local_step, mesh=mesh,
                          in_specs=(row_spec, row_spec, full_spec, full_spec, full_spec, full_spec, full_spec),

time: 44.8 us -> 36.9 us (0.82)
  local copies, waits for them, and re-layouts: 6.04 us -> 0 us
  other arithmetic: 2.54 us -> 0 us
  Pallas kernels: 35.4 us -> 36.2 us
    unnamed x13 -> x0, local copies, waits for them, and re-layouts: 6.04 us -> none
    pallas_call x2 -> x0, other arithmetic: 2.54 us -> none  [local_step(): pl.pallas_call(functools.partial(kernel, h, num_sp), name='xca', out_shap...]
    pallas_call x0 -> x1, Pallas kernels: none -> 2.45 us  [local_step(): pl.pallas_call(finish, name='finish', out_shape=(sds((n, d), BF16), sds((...]
    pallas_call x1, Pallas kernels: 35.4 us -> 33.7 us  [local_step(): pl.pallas_call(functools.partial(kernel, h, num_sp), name='xca', out_shap...]
where the time goes in v2:
time: 36.9 us; the launch traced here: 36.8 us
  Pallas kernels  36.2 us (98%)
  between operations  0.64 us (2%)
    pallas_call x1, Pallas kernels, local_step(): pl.pallas_call(functools.partial(kernel, h, num_sp), name='xca', out_shap...  33.7 us
    pallas_call x1, Pallas kernels, local_step(): pl.pallas_call(finish, name='finish', out_shape=(sds((n, d), BF16), sds((...  2.45 us

profile of v2, /device:TPU:0, one launch (start us, length us, event | category | flops | bytes accessed | tf_op | source)
XLA Modules:
  0.0 36.8 jit_solution(12241486621436004411)
XLA Ops:
  0.6 33.7 %xca.1 = (bf16[2048,384]{1,0:T(8,128)(2,1)S(1)}, bf16[2048,384]{1,0:T(8,128)(2,1)S(1)}, f32[96,1152]{1,0:T(8,128)S(1)}, f32[96,384]{1,0:T(8,128)S(1)}, f32[1,384...) custom-call(bf16[2048,384]{1,0:T(8,128)(2,1)} %x_hbm.1, bf16[2048,384]{1,0:T(8,128)(2,1)} %dy_hbm.1, ...), custom_call_target="tpu_custom_call" | custom-call | tf_op jit(solution)/shard_map/xca/pallas_call | solution.py:357
  34.4 2.4 %finish.1 = (bf16[2048,384]{1,0:T(8,128)(2,1)}, bf16[2048,384]{1,0:T(8,128)(2,1)}, f32[96,1152]{1,0:T(8,128)}, f32[96,384]{1,0:T(8,128)}, f32[384]{0:T(512)}, /*index=5*/f32[384]{0:T(512)}, f32[8]{0:T(128)}) custom-call(bf16[2048,384]{1,0:T(8,128)(2,1)S(1)} %get-tuple-element.14.out_v, bf16[2048,384]{1,0:T(8,128)(2,1)S(1)} %get-tuple-element.15.gt_v, ...), custom_call_target="tpu_custom_call" | custom-call | tf_op jit(solution)/shard_map/finish/pallas_call | solution.py:380

commit v3 on v0

v3 whole, which is shorter than its diff:
```python
import functools

import jax
import jax.numpy as jnp
from jax import lax
from jax.experimental import pallas as pl
from jax.experimental.pallas import tpu as pltpu
from jax.sharding import PartitionSpec as P

F32, BF16 = jnp.float32, jnp.bfloat16
MESH = pl.DeviceIdType.MESH
BM = 512
CHUNKS = ((2, 0, 128), (2, 128, 384), (3, 0, 384), (0, 0, 384), (1, 0, 384))
scope = jax.named_scope


def dot_nn(a, b):
    return lax.dot_general(a, b, (((1,), (0,)), ((), ())), preferred_element_type=F32)


def dot_nt(a, b):
    return lax.dot_general(a, b, (((1,), (1,)), ((), ())), preferred_element_type=F32)


def dot_tn(a, b):
    return lax.dot_general(a, b, (((0,), (0,)), ((), ())), preferred_element_type=F32)


def kernel(num_heads, num_sp,
           x_hbm, dy_hbm, gain_hbm, bias_hbm, wqkv_hbm, wout_hbm, temp_hbm,
           out_st, gt_st, gwqkv_ref, gwout_ref, ggain_ref, gbias_ref, gtemp_ref,
           gain_ref, bias_ref, temp_ref, x_v, dy_v, wqkv, wout, u_v, ut_v, xhat, rstd, q_v, k_v, v_v, do_v, o_v, dqkv,
           acc, abd, gbd, g_own, g_rx1, g_sum, g_rx2, d_own, d_rx1, d_sum, d_rx2,
           gw, w_rx1, w_sum, w_rx2, gb,
           in_sem, gs, gr, ws, wr, bs, br):
    rows_n, dim = x_v.shape
    hd = dim // num_heads
    nb = rows_n // BM
    wrows = dim // num_sp
    half = dim // 2
    win = 256
    off = dim - win
    nh = num_heads // 2

    me = lax.axis_index('sp')
    partner = me + 1 - 2 * lax.rem(me, 2)
    peer = lax.rem(me + 2, 4)
    diag = lax.rem(partner + 2, 4)

    def blk(i):
        return slice(i * BM, (i + 1) * BM)

    x_copy = [pltpu.make_async_copy(x_hbm.at[blk(i)], x_v.at[blk(i)], in_sem.at[i]) for i in range(nb)]
    dy_copy = pltpu.make_async_copy(dy_hbm, dy_v, in_sem.at[nb])
    wq_copy = pltpu.make_async_copy(wqkv_hbm, wqkv, in_sem.at[nb + 1])
    wo_copy = pltpu.make_async_copy(wout_hbm, wout, in_sem.at[nb + 2])
    small = [pltpu.make_async_copy(a, b, in_sem.at[nb + 3 + n]) for n, (a, b) in enumerate(
        ((gain_hbm, gain_ref), (bias_hbm, bias_ref), (temp_hbm, temp_ref)))]
    x_copy[0].start()
    for c in small:
        c.start()
    wq_copy.start()
    for i in range(1, nb):
        x_copy[i].start()
    wo_copy.start()
    dy_copy.start()

    barrier = pltpu.get_barrier_semaphore()
    for other in (partner, peer, diag):
        pl.semaphore_signal(barrier, inc=1, device_id={'sp': other}, device_id_type=MESH)

    lane = lax.broadcasted_iota(jnp.int32, (hd, dim), 1)
    row = lax.broadcasted_iota(jnp.int32, (hd, dim), 0)
    head_mask = [(lane >= h * hd) & (lane < (h + 1) * hd) for h in range(num_heads)]

    def fold(a):
        lo = jnp.zeros((hd, win), F32)
        hi = jnp.zeros((hd, win), F32)
        for h in range(nh):
            r = slice(h * hd, (h + 1) * hd)
            lo = jnp.where(head_mask[h][:, :win], a[0, r, :], lo)
            hi = jnp.where(head_mask[h + nh][:, off:], a[1, r, :], hi)
        return jnp.concatenate([lo[:, :off], lo[:, off:] + hi[:, :win - off], hi[:, win - off:]], axis=1)

    def expand(ref, compact):
        ref[0, half:, :] = jnp.zeros((win - half, win), BF16)
        ref[1, :half - off, :] = jnp.zeros((half - off, win), BF16)
        for h in range(nh):
            ref[0, h * hd:(h + 1) * hd, :] = jnp.where(head_mask[h], compact, 0.0).astype(BF16)[:, :win]
            g = h + nh
            r = slice(g * hd - off, (g + 1) * hd - off)
            ref[1, r, :] = jnp.where(head_mask[g], compact, 0.0).astype(BF16)[:, off:]

    def per_head(dot, a, w):
        lo = dot(a[:, :win], w[0])
        hi = dot(a[:, off:], w[1])
        return jnp.concatenate([lo[:, :off], lo[:, off:] + hi[:, :win - off], hi[:, win - off:]], axis=1)

    def head_gram(a, b, first):
        at = a.T
        lo = dot_nn(at[:half], b[:, :win])
        hi = dot_nn(at[half:], b[:, off:])
        if first:
            acc[0] = lo
            acc[1] = hi
        else:
            acc[0] += lo
            acc[1] += hi

    def send(src, dst, ssem, rsem, dev):
        return pltpu.make_async_remote_copy(src_ref=src, dst_ref=dst, send_sem=ssem, recv_sem=rsem,
                                            device_id={'sp': dev}, device_id_type=MESH)

    for c in small:
        c.wait()
    gain = gain_ref[...].reshape(1, dim)
    bias = bias_ref[...].reshape(1, dim)
    inv_d = 1.0 / dim

    def layer_norm(i):
        r = blk(i)
        xf = x_v[r, :].astype(F32)
        cen = xf - jnp.sum(xf, axis=-1, keepdims=True) * inv_d
        var = jnp.sum(cen * cen, axis=-1, keepdims=True) * inv_d
        rs = lax.rsqrt(var + 1e-6)
        xh = cen * rs
        xhat[r, :] = xh
        rstd[r, :] = jnp.broadcast_to(rs, (BM, 128))
        u_v[r, :] = (xh * gain + bias).astype(BF16)

    def project_qk(i):
        r = blk(i)
        qk = dot_nn(u_v[r, :], wqkv[:, :2 * dim]).astype(BF16)
        q_v[r, :] = qk[:, :dim]
        k_v[r, :] = qk[:, dim:]

    def sq_sum(ref, i):
        f = ref[blk(i), :].astype(F32)
        return jnp.sum((f * f).reshape(BM // 8, 8, dim), axis=0)

    sq = sk = jnp.zeros((8, dim), F32)
    with scope('p1'):
        x_copy[0].wait()
        layer_norm(0)
        wq_copy.wait()
        for i in range(nb + 1):
            if i + 1 < nb:
                x_copy[i + 1].wait()
                layer_norm(i + 1)
            if i < nb:
                project_qk(i)
            if i > 0:
                head_gram(k_v[blk(i - 1), :], q_v[blk(i - 1), :], i == 1)
                sq = sq + sq_sum(q_v, i - 1)
                sk = sk + sq_sum(k_v, i - 1)
    with scope('fold'):
        g_own[:hd, :] = fold(acc)
        row8 = lax.broadcasted_iota(jnp.int32, (8, dim), 0)
        g_own[hd:hd + 8, :] = jnp.where(row8 == 0, jnp.sum(sq, axis=0, keepdims=True),
                                        jnp.where(row8 == 1, jnp.sum(sk, axis=0, keepdims=True), 0.0))
    pl.semaphore_wait(barrier, 3)
    g1 = send(g_own, g_rx1, gs.at[0], gr.at[0], partner)
    g1.start()

    def p2(i):
        r = blk(i)
        u = u_v[r, :]
        ut_v[:, r] = u.T
        v_v[r, :] = dot_nn(u, wqkv[:, 2 * dim:]).astype(BF16)
        do_v[r, :] = dot_nt(dy_v[r, :], wout[...]).astype(BF16)

    with scope('p2a'):
        wo_copy.wait()
        dy_copy.wait()
        for i in range(nb // 2):
            p2(i)
    with scope('g1w'):
        g1.wait()
    g_sum[...] = g_own[...] + g_rx1[...]
    g2 = send(g_sum, g_rx2, gs.at[1], gr.at[1], peer)
    g2.start()
    with scope('p2b'):
        for i in range(nb // 2, nb):
            p2(i)
        for i in range(nb):
            head_gram(v_v[blk(i), :], do_v[blk(i), :], i == 0)
    d_own[...] = fold(acc)
    d1 = send(d_own, d_rx1, gs.at[2], gr.at[2], partner)
    d1.start()

    with scope('g2w'):
        g2.wait()
    with scope('A'):
        tot = g_sum[...] + g_rx2[...]
        gram = tot[:hd, :]
        sq_row = tot[hd:hd + 1, :]
        sk_row = tot[hd + 1:hd + 2, :]
        sk_full = jnp.zeros((hd, dim), F32)
        for h in range(num_heads):
            col = jnp.sum(jnp.where(lane == row + h * hd, sk_row, 0.0), axis=1, keepdims=True)
            sk_full = jnp.where(head_mask[h], col, sk_full)
        tau = jnp.zeros((1, dim), F32)
        for h in range(num_heads):
            tau = jnp.where(head_mask[h][:1, :], temp_ref[h], tau)
        denom = jnp.sqrt(sq_row) * jnp.sqrt(sk_full)
        cos = gram / denom
        s = tau * cos
        e = jnp.exp(s - jnp.max(s, axis=0, keepdims=True))
        prob = e / jnp.sum(e, axis=0, keepdims=True)
        expand(abd, prob)

    def pair_send(n, part):
        c, lo, hi = CHUNKS[n]
        rows = pl.ds(pl.multiple_of((partner if part else diag) * wrows, 8), wrows)
        return send(gw.at[c, rows, lo:hi], w_rx1.at[c, part, :, lo:hi], ws.at[3 * n + part], wr.at[3 * n + part], partner)

    def cross_send(n):
        c, lo, hi = CHUNKS[n]
        return send(w_sum.at[c, :, lo:hi], w_rx2.at[c, :, lo:hi], ws.at[3 * n + 2], wr.at[3 * n + 2], peer)

    def pair_start(n):
        pair_send(n, 0).start()
        pair_send(n, 1).start()

    def cross_start(n):
        c, lo, hi = CHUNKS[n]
        with scope(f'cs{n}'):
            pair_send(n, 0).wait()
            rows = pl.ds(pl.multiple_of(peer * wrows, 8), wrows)
            w_sum[c, :, lo:hi] = gw[c, rows, lo:hi] + w_rx1[c, 0, :, lo:hi]
            cross_send(n).start()

    with scope('p3'):
        dqkv[:, 2 * dim:] = per_head(dot_nt, do_v[...], abd).astype(BF16)
    with scope('gw2a'):
        gw[2, :, :128] = dot_nn(ut_v[...], dqkv[:, 2 * dim:2 * dim + 128])
    pair_start(0)
    with scope('d1w'):
        d1.wait()
    d_sum[...] = d_own[...] + d_rx1[...]
    d2 = send(d_sum, d_rx2, gs.at[3], gr.at[3], peer)
    d2.start()
    with scope('gw2b'):
        gw[2, :, 128:] = dot_nn(ut_v[...], dqkv[:, 2 * dim + 128:])
    pair_start(1)
    cross_start(0)

    with scope('p4'):
        o_v[...] = per_head(dot_nn, v_v[...], abd).astype(BF16)
    cross_start(1)
    with scope('gw3'):
        gw[3] = dot_tn(o_v[...], dy_v[...])
    pair_start(2)

    with scope('d2w'):
        d2.wait()
    with scope('dA'):
        da = d_sum[...] + d_rx2[...]
        ds = prob * (da - jnp.sum(prob * da, axis=0, keepdims=True))
        dcos = tau * ds
        t_row = jnp.sum(ds * cos, axis=0, keepdims=True)
        lane_t = lax.broadcasted_iota(jnp.int32, (1, num_heads), 1)
        g_temp = jnp.zeros((1, num_heads), F32)
        for h in range(num_heads):
            val = jnp.sum(jnp.where(head_mask[h][:1, :], t_row, 0.0), axis=1, keepdims=True)
            g_temp = jnp.where(lane_t == h, val, g_temp)
        gtemp_ref[...] = g_temp.reshape(num_heads)
        expand(gbd, dcos / denom)
        z = dcos * cos
        dsq2 = -jnp.sum(z, axis=0, keepdims=True) / sq_row
        sk_grad = jnp.zeros((hd, dim), F32)
        for h in range(num_heads):
            col = jnp.sum(jnp.where(head_mask[h], z, 0.0), axis=1, keepdims=True)
            sk_grad = jnp.where(lane == row + h * hd, col, sk_grad)
        dsk2 = -jnp.sum(sk_grad, axis=0, keepdims=True) / sk_row

    with scope('p5'):
        dqkv[:, :dim] = (per_head(dot_nn, k_v[...], gbd) + q_v[...].astype(F32) * dsq2).astype(BF16)
    cross_start(2)
    with scope('gw0'):
        gw[0] = dot_nn(ut_v[...], dqkv[:, :dim])
    pair_start(3)
    with scope('p6'):
        dqkv[:, dim:2 * dim] = (per_head(dot_nt, q_v[...], gbd) + k_v[...].astype(F32) * dsk2).astype(BF16)
    cross_start(3)
    with scope('gw1'):
        gw[1] = dot_nn(ut_v[...], dqkv[:, dim:2 * dim])
    pair_start(4)

    with scope('p7'):
        for i in range(nb):
            r = blk(i)
            out_st[r, :] = (x_v[r, :].astype(F32) + dot_nn(o_v[r, :], wout[...])).astype(BF16)
    cross_start(4)

    def p8(i, carry):
        gg, gbi = carry
        r = pl.ds(pl.multiple_of(i * BM, BM), BM)
        du = dot_nt(dqkv[r, :], wqkv[...])
        xh = xhat[r, :]
        dux = du * xh
        gg = gg + jnp.sum(dux.reshape(BM // 8, 8, dim), axis=0)
        gbi = gbi + jnp.sum(du.reshape(BM // 8, 8, dim), axis=0)
        m1 = jnp.sum(du * gain, axis=-1, keepdims=True) * inv_d
        m2 = jnp.sum(dux * gain, axis=-1, keepdims=True) * inv_d
        dx = (du * gain - m1 - xh * m2) * rstd[r, :1]
        gt_st[r, :] = (dy_v[r, :].astype(F32) + dx).astype(BF16)
        return gg, gbi

    with scope('p8'):
        zero8 = jnp.zeros((8, dim), F32)
        gg, gbi = lax.fori_loop(0, nb, p8, (zero8, zero8))
        gb[me] = jnp.where(row8 == 0, jnp.sum(gg, axis=0, keepdims=True),
                           jnp.where(row8 == 1, jnp.sum(gbi, axis=0, keepdims=True), 0.0))
    gbc = [send(gb.at[me], gb.at[me], bs.at[n], br.at[n], other) for n, other in enumerate((partner, peer, diag))]
    for c in gbc:
        c.start()

    mine = pl.ds(pl.multiple_of(me * wrows, 8), wrows)
    for n, (c, lo, hi) in enumerate(CHUNKS):
        with scope(f'fin{n}'):
            pair_send(n, 1).wait()
            cross_send(n).wait()
        total = gw[c, mine, lo:hi] + w_rx1[c, 1, :, lo:hi] + w_rx2[c, :, lo:hi]
        if c == 3:
            gwout_ref[:, lo:hi] = total
        else:
            gwqkv_ref[:, c * dim + lo:c * dim + hi] = total
    with scope('gbw'):
        for c in gbc:
            c.wait()
    gsum = (gb[0] + gb[1]) + (gb[2] + gb[3])
    ggain_ref[...] = gsum[0:1, :].reshape(dim)
    gbias_ref[...] = gsum[1:2, :].reshape(dim)


def finish(*refs):
    count = (len(refs) - 1) // 2
    sem = refs[-1]
    copies = [pltpu.make_async_copy(refs[n], refs[count + n], sem.at[n]) for n in range(count)]
    for c in copies:
        c.start()
    for c in copies:
        c.wait()


def solution(mesh):
    row_spec = P(('dp', 'sp'), None)
    part_spec = P('dp')
    full_spec = P()
    num_sp = mesh.shape['sp']

    def local_step(x, dy, gain, bias, w_qkv, w_out, temperature):
        n, d = x.shape
        h = temperature.shape[0]
        hd = d // h
        wrows = d // num_sp
        nb = n // BM
        vmem = pl.BlockSpec(memory_space=pltpu.VMEM)
        hbm = pl.BlockSpec(memory_space=pltpu.HBM)
        tok = pltpu.VMEM((n, d), BF16)
        dma = pltpu.SemaphoreType.DMA
        in_hbm = functools.partial(pltpu.with_memory_space_constraint, memory_space=pltpu.HBM)
        shapes = (((n, d), BF16), ((n, d), BF16), ((wrows, 3 * d), F32), ((wrows, d), F32),
                  ((d,), F32), ((d,), F32), ((h,), F32))
        wide = pltpu.VMEM((hd + 8, d), F32)
        slim = pltpu.VMEM((hd, d), F32)
        outs = pl.pallas_call(
            functools.partial(kernel, h, num_sp),
            name='xca',
            out_shape=tuple(pltpu.VMEM(*s) for s in shapes),
            in_specs=[hbm] * 7,
            out_specs=(vmem,) * 7,
            scratch_shapes=[
                pltpu.VMEM((d,), F32), pltpu.VMEM((d,), F32), pltpu.SMEM((h,), F32),
                tok, tok, pltpu.VMEM((d, 3 * d), BF16), pltpu.VMEM((d, d), BF16), tok, pltpu.VMEM((d, n), BF16),
                pltpu.VMEM((n, d), F32), pltpu.VMEM((n, 128), F32), tok, tok, tok, tok, tok,
                pltpu.VMEM((n, 3 * d), BF16),
                pltpu.VMEM((2, d // 2, 256), F32), pltpu.VMEM((2, 256, 256), BF16), pltpu.VMEM((2, 256, 256), BF16),
                wide, wide, wide, wide, slim, slim, slim, slim,
                pltpu.VMEM((4, d, d), F32), pltpu.VMEM((4, 2, wrows, d), F32), pltpu.VMEM((4, wrows, d), F32),
                pltpu.VMEM((4, wrows, d), F32), pltpu.VMEM((4, 8, d), F32),
                dma((nb + 6,)), dma((4,)), dma((4,)),
                dma((3 * len(CHUNKS),)), dma((3 * len(CHUNKS),)), dma((3,)), dma((3,)),
            ],
            compiler_params=pltpu.CompilerParams(collective_id=0, has_side_effects=True,
                                                 vmem_limit_bytes=44 * 1024 * 1024),
        )(*map(in_hbm, (x, dy, gain, bias, w_qkv, w_out, temperature)))
        return pl.pallas_call(
            finish,
            name='finish',
            out_shape=tuple(jax.ShapeDtypeStruct(*s) for s in shapes),
            in_specs=[vmem] * 7,
            out_specs=(hbm,) * 7,
            scratch_shapes=[dma((7,))],
            compiler_params=pltpu.CompilerParams(vmem_limit_bytes=8 * 1024 * 1024),
        )(*outs)

    return jax.shard_map(local_step, mesh=mesh,
                         in_specs=(row_spec, row_spec, full_spec, full_spec, full_spec, full_spec, full_spec),
                         out_specs=(row_spec, row_spec, row_spec, row_spec, part_spec, part_spec, part_spec),
                         check_vma=False)
```

time: 142 us -> 32.2 us (0.23)
  matrix products: 49.8 us -> 0 us
  waiting for transfers between devices: 36.3 us -> 0 us
  Pallas kernels: 0 us -> 31.4 us
  other arithmetic: 19.8 us -> 0 us
  blocking collectives: 15.9 us -> 0 us
  between operations: 14.1 us -> 0.64 us
  local copies, waits for them, and re-layouts: 5.98 us -> 0 us
    dot_general x14 -> x0, matrix products: 49.8 us -> none  [the longest x2 8.22 us: project(): jnp.dot(normed, w_qkv, preferred_element_type=jnp.float32)]
    psum x2 -> x0, waiting for transfers between devices: 34.3 us -> none  [the longest x1 18.4 us: local_step(): d_probs = lax.psum(probs_part, 'sp')]
    pallas_call x0 -> x2, Pallas kernels: none -> 31.4 us  [the longest x1 29.5 us: local_step(): pl.pallas_call(functools.partial(kernel, h, num_sp), name='xca', out_shap...]
    psum x2 -> x0, blocking collectives: 15.9 us -> none  [the longest x1 9.07 us: local_step(): gram_sum, q_sq, k_sq = lax.psum((gram_part, qsq_part, ksq_part), 'sp')]
    reduce_sum x7 -> x0, other arithmetic: 8.8 us -> none  [the longest x2 3.02 us: layer_norm(): row_var = jnp.mean(centered * centered, axis=-1, keepdims=True)]
    unnamed x26 -> x0, local copies, waits for them, and re-layouts: 5.96 us -> none
    convert_element_type x1 -> x0, other arithmetic: 5 us -> none  [local_step(): grad_tokens = (dy_loc.astype(jnp.float32) + d_x).astype(jnp.bfloat16)]
    sub x2 -> x0, other arithmetic: 3.51 us -> none  [attn_probs(): return jax.nn.softmax(value_a11[..., None, None] * cosine, axis=-1)]
  transfers between devices with their start and end apart: 4 -> 0, of which waited for: 3 -> 0; matrix products, arithmetic and copies ran while one was open for 32% -> 0% of each run, Pallas kernels for 0% -> 0%
where the time goes in v3:
time: 32.2 us; the launch traced here: 32.1 us
  Pallas kernels  31.4 us (98%)
  between operations  0.64 us (2%)
    pallas_call x1, Pallas kernels, local_step(): pl.pallas_call(functools.partial(kernel, h, num_sp), name='xca', out_shap...  29.5 us
    pallas_call x1, Pallas kernels, local_step(): pl.pallas_call(finish, name='finish', out_shape=tuple((jax.ShapeDtypeStru...  1.91 us

profile of v3, /device:TPU:0, one launch (start us, length us, event | category | flops | bytes accessed | tf_op | source)
XLA Modules:
  0.0 32.1 jit_solution(4060984410272347050)
XLA Ops:
  0.6 29.5 %xca.1 = (bf16[2048,384]{1,0:T(8,128)(2,1)S(1)}, bf16[2048,384]{1,0:T(8,128)(2,1)S(1)}, f32[96,1152]{1,0:T(8,128)S(1)}, f32[96,384]{1,0:T(8,128)S(1)}, f32[384]{...) custom-call(bf16[2048,384]{1,0:T(8,128)(2,1)} %x_hbm.1, bf16[2048,384]{1,0:T(8,128)(2,1)} %dy_hbm.1, f32[384]{0:T(512)} %gain_hbm.1, ...), custom_call_target="tpu_custom_call" | custom-call | tf_op jit(solution)/shard_map/xca/pallas_call | solution.py:368
  30.2 1.9 %finish.1 = (bf16[2048,384]{1,0:T(8,128)(2,1)}, bf16[2048,384]{1,0:T(8,128)(2,1)}, f32[96,1152]{1,0:T(8,128)}, f32[96,384]{1,0:T(8,128)}, f32[384]{0:T(512)}, /*index=5*/f32[384]{0:T(512)}, f32[8]{0:T(128)}) custom-call(bf16[2048,384]{1,0:T(8,128)(2,1)S(1)} %get-tuple-element.14.refs_0_, bf16[2048,384]{1,0:T(8,128)(2,1)S(1)} %get-tuple-element.15.refs_1_, ...), custom_call_target="tpu_custom_call" | custom-call | tf_op jit(solution)/shard_map/finish/pallas_call | solution.py:389
